TPU v7x, 256 devices: a whole 4x4x8 slice. The times are simulated.
256 devices in a mesh: dp: 64 (over z, y, core), vocab: 4 (over x).
Axes of the slice: x: 4, y: 4, z: 8, core: 2. Of those that a mesh axis runs over, the one named last changes fastest.
Arguments:
- hidden_in: bfloat16 [512, 24, 1024], P(('dp', 'vocab')), may hold values from -6 to 6
- tokens: int32 [512, 24], P(('dp', 'vocab')), may hold values from 0 to 131071
- lengths: int32 [512], P(('dp', 'vocab')), may hold values from 2 to 24, as said below
- cutoff: int32 [1], replicated, may hold values from 1 to 512
- norm_gain: float32 [1024], replicated, may hold values from 0.5 to 1.5
- gate_weight: bfloat16 [1024, 4096], P(None, 'vocab'), may hold values from -0.1875 to 0.1875
- up_weight: bfloat16 [1024, 4096], P(None, 'vocab'), may hold values from -0.1875 to 0.1875
- down_weight: bfloat16 [4096, 1024], P('vocab'), may hold values from -0.09375 to 0.09375
- final_gain: float32 [1024], replicated, may hold values from 0.5 to 1.5
- head_table: bfloat16 [131072, 1024], P(('dp', 'vocab')), may hold values from -12 to 12
Outputs:
- log_ppl: float32 [512], P(('dp', 'vocab'))
- margin: float32 [512], P(('dp', 'vocab'))
Inputs may be any that keep to these rules, and one draw needn't show every extreme that they name: Every length is 2 or more; the documents of one device have together at most 32 positions below their lengths, and some device has exactly 32.
All inputs are finite; a program needn't handle non-finite values.
Results may differ from a plain program's by a relative error of at most 0.025.
Values may be sent and summed in bfloat16 or wider, within the bound.
No kernel may reach another device: no remote copies, remote signals or barrier semaphores. Data moves between devices by JAX's collectives and lax.ppermute only.
A program may use at most 64 MiB of HBM per device.

v0:
```python
import jax
import jax.numpy as jnp
from jax import lax
from jax.sharding import Mesh
from jax.sharding import PartitionSpec as P

CAP = 32
DP = ("dp_0", "dp_1", "dp_2")
DP_VOCAB = ("dp_0", "dp_1", "dp_2", "vocab")


def copy_for_each(array, axis):
    length = lax.axis_size(axis)
    return lax.all_to_all(
        jnp.broadcast_to(array[None], (length, *array.shape)), axis, 0, 0, tiled=True
    )


def joined_along(parts, dim):
    parts = jnp.moveaxis(parts, 0, dim)
    lengths = parts.shape
    return parts.reshape(*lengths[:dim], lengths[dim] * lengths[dim + 1], *lengths[dim + 2 :])


def gather_directly(array, axis, dim):
    parts = copy_for_each(array, axis)
    return joined_along(parts, dim)


def split_up(array, dim, length):
    lengths = array.shape
    parts = array.reshape(*lengths[:dim], length, lengths[dim] // length, *lengths[dim + 1 :])
    return jnp.moveaxis(parts, dim, 0)


def sum_at_owner(array, axis, dim):
    parts = split_up(array, dim, lax.axis_size(axis))
    arrived = lax.all_to_all(parts, axis, split_axis=0, concat_axis=0, tiled=True)
    return arrived.sum(axis=0)


def all_in_one(array, axis):
    leaves = jax.tree.leaves(array)
    order = sorted(range(len(leaves)), key=lambda k: -leaves[k].size)
    width = (1, *leaves[order[0]].shape)[-1]
    lines = [
        jnp.pad(leaves[k].reshape(-1), (0, -leaves[k].size % width)).reshape(-1, width)
        for k in order
    ]
    both, at, found = (lax.all_gather(jnp.concatenate(lines), axis), 0, {})
    for k, line in zip(order, lines):
        share = both[:, at : at + len(line)].reshape(len(both), -1)
        found[k] = share[:, : leaves[k].size].reshape(-1, *leaves[k].shape)
        at += len(line)
    numbers = iter(range(len(leaves)))
    return jax.tree.map(lambda _: found[next(numbers)], array)


def joined_all(array, axes, combine):
    for axis in axes:
        pieces = all_in_one(array, axis)
        array = jax.tree.map(lambda part: part[0], pieces)
        for k in range(1, lax.axis_size(axis)):
            array = combine(array, jax.tree.map(lambda part: part[k], pieces))
    return array


def gathered_by_axis(array, axes, dim):
    far, near = axes
    parts = copy_for_each(copy_for_each(array, far), near)
    return joined_along(parts.swapaxes(0, 1).reshape(-1, *array.shape), dim)


def rms_norm(values, gain):
    squares = jnp.mean(values * values, axis=-1, keepdims=True)
    return values * lax.rsqrt(squares + 1e-06) * gain


def block_rows(row_count, shard_rows):
    shards = row_count // shard_rows
    grouped = 1
    for divisor in range(1, shards + 1):
        if shards % divisor == 0 and divisor * shard_rows <= 768:
            grouped = divisor
    return grouped * shard_rows


def merge_pair(left_side, right_side):
    highest = jnp.maximum(left_side[0], right_side[0])
    exp_sum = left_side[1] * jnp.exp(left_side[0] - highest) + right_side[1] * jnp.exp(
        right_side[0] - highest
    )
    return (highest, exp_sum, left_side[2] + right_side[2])


def make_accumulate(table, offset, shard_rows, model_width):
    column = jnp.arange(table.shape[0], dtype=jnp.int32)

    def score_block(block_pair):
        block_part, block_targets = block_pair
        logits = lax.dot_general(
            block_part, table, (((1,), (1,)), ((), ())), preferred_element_type=jnp.float32
        )
        highest = jnp.max(logits, axis=1)
        exp_sum = jnp.sum(jnp.exp(logits - highest[:, None]), axis=1)
        local_index = block_targets - offset
        picked = jnp.sum(jnp.where(column[None, :] == local_index[:, None], logits, 0.0), axis=1)
        return (highest, exp_sum, picked)

    def accumulate(running, segment, first_row):
        segment_rows, segment_targets = segment
        row_count = segment_rows.shape[0]
        block_size = block_rows(row_count, shard_rows)
        blocks = row_count // block_size
        results = lax.map(
            score_block,
            (
                segment_rows.reshape(blocks, block_size, model_width),
                segment_targets.reshape(blocks, block_size),
            ),
        )
        return tuple((fresh.reshape(row_count) for fresh in results))

    return accumulate


def on_device(
    hidden_in,
    tokens,
    lengths,
    cutoff,
    norm_gain,
    gate_weight,
    up_weight,
    down_weight,
    final_gain,
    head_table,
):
    doc_count, length, model_width = hidden_in.shape
    row_total = doc_count * length
    residual = hidden_in.reshape(row_total, model_width).astype(jnp.float32)
    normed = rms_norm(residual, norm_gain).astype(jnp.bfloat16)
    segment = gather_directly(normed, "vocab", 0)
    gate_part = jnp.dot(segment, gate_weight, preferred_element_type=jnp.float32)
    up_part = jnp.dot(segment, up_weight, preferred_element_type=jnp.float32)
    active = (jax.nn.silu(gate_part) * up_part).astype(jnp.bfloat16)
    branch = sum_at_owner(
        jnp.dot(active, down_weight, preferred_element_type=jnp.float32), "vocab", 0
    )
    stream = (residual + branch).astype(jnp.bfloat16)
    final_rows = rms_norm(stream.astype(jnp.float32), final_gain).astype(jnp.bfloat16)
    targets = jnp.concatenate([tokens[:, 1:], tokens[:, :1]], axis=1).reshape(row_total)
    position = jnp.arange(length, dtype=jnp.int32)
    live_mask = (position[None, :] < lengths[:, None] - 1).reshape(row_total)
    slot_index = jnp.cumsum(live_mask.astype(jnp.int32)) - 1
    placing = (slot_index[None, :] == jnp.arange(CAP, dtype=jnp.int32)[:, None]) & live_mask[
        None, :
    ]
    send_rows = jnp.dot(
        placing.astype(jnp.bfloat16), final_rows, preferred_element_type=jnp.float32
    ).astype(jnp.bfloat16)
    send_targets = jnp.sum(jnp.where(placing, targets[None, :], 0), axis=1)
    shard_rows = send_rows.shape[0]
    joined_table = gather_directly(head_table, "vocab", 0)
    offset = lax.axis_index(DP) * joined_table.shape[0]
    accumulate = make_accumulate(joined_table, offset, shard_rows, model_width)
    dp_rows = shard_rows * lax.axis_size(DP)
    blank_dp = jnp.zeros((dp_rows,), jnp.float32)
    peaks, sums_exp, picks = accumulate(
        (blank_dp, blank_dp, blank_dp),
        (
            lax.all_gather(send_rows, DP, axis=0, tiled=True),
            lax.all_gather(send_targets, DP, axis=0, tiled=True),
        ),
        jnp.int32(0),
    )
    peaks, sums_exp, picks = joined_all((peaks, sums_exp, picks), DP, merge_pair)
    mine = lax.axis_index(DP) * shard_rows
    highest = lax.dynamic_slice_in_dim(peaks, mine, shard_rows, 0)
    exp_sum = lax.dynamic_slice_in_dim(sums_exp, mine, shard_rows, 0)
    target_logit = lax.dynamic_slice_in_dim(picks, mine, shard_rows, 0)
    nll_slots = highest + jnp.log(exp_sum) - target_logit
    nll_rows = jnp.sum(jnp.where(placing, nll_slots[:, None], 0.0), axis=0)
    used_nll = jnp.where(live_mask, nll_rows, 0.0).reshape(doc_count, length)
    log_ppl = jnp.sum(used_nll, axis=1) / (lengths - 1).astype(jnp.float32)
    everyone = gathered_by_axis(log_ppl, (("dp_0", "dp_1"), ("dp_2", "vocab")), 0)
    ordered = jnp.sort(everyone)
    threshold = lax.dynamic_index_in_dim(ordered, cutoff[0] - 1, 0, keepdims=False)
    return (log_ppl, log_ppl - threshold)


def solution(mesh):
    finer = Mesh(
        mesh.devices.reshape(8, 4, 2, mesh.shape["vocab"]), ("dp_0", "dp_1", "dp_2", "vocab")
    )
    return jax.shard_map(
        on_device,
        mesh=finer,
        in_specs=(
            P(DP_VOCAB, None, None),
            P(DP_VOCAB, None),
            P(DP_VOCAB),
            P(),
            P(),
            P(None, "vocab"),
            P(None, "vocab"),
            P("vocab", None),
            P(),
            P(DP_VOCAB, None),
        ),
        out_specs=(P(DP_VOCAB), P(DP_VOCAB)),
        check_vma=False,
    )
```

profile of v0, /device:TPU:1, one launch (start us, length us, event | category | flops | bytes accessed | tf_op | source)
XLA Modules:
  0.0 228.5 jit_solution(5545836464481347392)
XLA Ops:
  7.2 1.1 fusion.14
  8.4 1.0 fusion.17
  9.5 11.8 %all_to_all.26 = bf16[4,48,1024]{2,1,0:T(8,128)(2,1)S(1)} all-to-all(bf16[4,48,1024]{2,1,0:T(8,128)(2,1)S(1)} %broadcast_in_dim.82), channel_id=1, replica_groups=mesh['dp_0'=8,'dp_1'=4,'dp_2'=2,'vocab'=4] {'vocab'}, dimensions={0} | all-to-all | bytes 786432 | tf_op jit(solution)/shard_map/all_to_all | solution.py:14
  21.3 0.6 fusion.78
  21.9 4.3 %fusion.7 = f32[192,1024]{1,0:T(8,128)} fusion(bf16[1024,1024]{1,0:T(8,128)(2,1)} %param.19, bf16[192,1024]{1,0:T(8,128)(2,1)S(1)} %bitcast.305, bf16[1024,1024]{1,0:T(8,128)(2,1)} %param.18, f32[192,1024]{1,0:T(8,128)S(1)} %fusion.78), kind=kOutput, calls=%fused_computation.11 | convolution fusion | flops 806486016 | bytes 6160384 | tf_op jit(solution)/shard_map/dot_general | solution.py:148
  26.2 3.5 %all-to-all-start.1 = ((f32[4,48,1024]{2,1,0:T(8,128)}), f32[4,48,1024]{2,1,0:T(8,128)S(1)}, u32[]{:S(2)}, u32[]{:S(2)}) async-start(f32[4,48,1024]{2,1,0:T(8,128)} %bitcast.306), calls=%async_computation.1 | async-start | bytes 1572864 | tf_op jit(solution)/shard_map/all_to_all | solution.py:38
  30.2 9.7 %all-to-all-done.1 = f32[4,48,1024]{2,1,0:T(8,128)S(1)} async-done(((f32[4,48,1024]{2,1,0:T(8,128)}), f32[4,48,1024]{2,1,0:T(8,128)S(1)}, u32[]{:S(2)}, u32[]{:S(2)}) %all-to-all-start.1) | async-done | bytes 786464 | tf_op jit(solution)/shard_map/all_to_all | solution.py:38
  40.2 0.9 convolution_convert_fusion
  41.1 3.7 %broadcast_in_dim.83 = bf16[4,512,1024]{2,1,0:T(8,128)(2,1)} broadcast(bf16[512,1024]{1,0:T(8,128)(2,1)} %param.21), dimensions={1,2} | broadcast | bytes 5242880 | tf_op jit(solution)/shard_map/broadcast_in_dim | solution.py:15
  44.9 5.0 %all-to-all-start.2 = ((bf16[4,512,1024]{2,1,0:T(8,128)(2,1)}), bf16[4,512,1024]{2,1,0:T(8,128)(2,1)}, u32[]{:S(2)}, u32[]{:S(2)}) async-start(bf16[4,512,1024]{2,1,0:T(8,128)(2,1)} %broadcast_in_dim.83), calls=%async_computation.2 | async-start | bytes 8388608 | tf_op jit(solution)/shard_map/all_to_all | solution.py:14
  51.8 23.7 %all-reduce = s32[2048]{0:T(1024)S(1)} all-reduce(s32[2048]{0:T(1024)S(1)} %dynamic-update-slice), channel_id=1, replica_groups=mesh['dp_0'=8,'dp_1'=4,'dp_2'=2,'vocab'=4] {'dp_0','dp_1','dp_2'}, use_global_device_ids=true, to_apply=%add | all-reduce | flops 2048 | bytes 16384
  75.5 20.4 %all-to-all-done.2 = bf16[4,512,1024]{2,1,0:T(8,128)(2,1)} async-done(((bf16[4,512,1024]{2,1,0:T(8,128)(2,1)}), bf16[4,512,1024]{2,1,0:T(8,128)(2,1)}, u32[]{:S(2)}, u32[]{:S(2)}) %all-to-all-start.2) | async-done | bytes 4194336 | tf_op jit(solution)/shard_map/all_to_all | solution.py:14
  95.8 28.5 %all-gather.8.cloned.1.call-done = bf16[2048,1024]{1,0:T(8,128)(2,1)} async-done(((bf16[32,1024]{1,0:T(8,128)(2,1)}), bf16[2048,1024]{1,0:T(8,128)(2,1)}) %all-gather.8.cloned.1.call-update) | async-done | bytes 4194320 | tf_op jit(solution)/shard_map/all_gather | solution.py:172
  124.3 26.3 %while.15 = (s32[]{:T(128)}, f32[4,512]{1,0:T(4,128)S(1)}, f32[4,512]{1,0:T(4,128)S(1)}, f32[4,512]{1,0:T(4,128)S(1)}, bf16[4,512,1024]{2,1,0:T(8,128)(2,1)}, /*...) while((s32[]{:T(128)}, f32[4,512]{1,0:T(4,128)S(1)}, ...), condition=%wide.region_9.10_spmd.clone, body=%wide.region_5.9_spmd.clone.sunk | while | flops 2153774080 | bytes 13658745 | solution.py:115
  124.3 5.0 %fusion.88 = (f32[512]{0:T(512)S(1)}, f32[512,2048]{1,0:T(8,128)S(1)}) fusion(bf16[2048,1024]{1,0:T(8,128)(2,1)} %get-tuple-element.189, bf16[4,512,1024]{2,1,0:T(8,128)(2,1)} %get-tuple-element.188, s32[]{:T(128)} %get-tuple-element.174), kind=kOutput, calls=%fused_computation.138.clone.1 | convolution fusion | flops 2148531712 | bytes 9439744 | tf_op jit(solution)/shard_map/while/body/eval_jaxpr/dot_general | solution.py:101
  129.3 1.4 select_reduce_fusion.5
  130.9 5.0 %fusion.88 = (f32[512]{0:T(512)S(1)}, f32[512,2048]{1,0:T(8,128)S(1)}) fusion(bf16[2048,1024]{1,0:T(8,128)(2,1)} %get-tuple-element.189, bf16[4,512,1024]{2,1,0:T(8,128)(2,1)} %get-tuple-element.188, s32[]{:T(128)} %get-tuple-element.174), kind=kOutput, calls=%fused_computation.138.clone.1 | convolution fusion | flops 2148531712 | bytes 9439744 | tf_op jit(solution)/shard_map/while/body/eval_jaxpr/dot_general | solution.py:101
  135.9 1.4 select_reduce_fusion.5
  137.5 5.0 %fusion.88 = (f32[512]{0:T(512)S(1)}, f32[512,2048]{1,0:T(8,128)S(1)}) fusion(bf16[2048,1024]{1,0:T(8,128)(2,1)} %get-tuple-element.189, bf16[4,512,1024]{2,1,0:T(8,128)(2,1)} %get-tuple-element.188, s32[]{:T(128)} %get-tuple-element.174), kind=kOutput, calls=%fused_computation.138.clone.1 | convolution fusion | flops 2148531712 | bytes 9439744 | tf_op jit(solution)/shard_map/while/body/eval_jaxpr/dot_general | solution.py:101
  142.4 1.4 select_reduce_fusion.5
  144.0 5.0 %fusion.88 = (f32[512]{0:T(512)S(1)}, f32[512,2048]{1,0:T(8,128)S(1)}) fusion(bf16[2048,1024]{1,0:T(8,128)(2,1)} %get-tuple-element.189, bf16[4,512,1024]{2,1,0:T(8,128)(2,1)} %get-tuple-element.188, s32[]{:T(128)} %get-tuple-element.174), kind=kOutput, calls=%fused_computation.138.clone.1 | convolution fusion | flops 2148531712 | bytes 9439744 | tf_op jit(solution)/shard_map/while/body/eval_jaxpr/dot_general | solution.py:101
  149.0 1.4 select_reduce_fusion.5
  150.7 18.4 %all-gather.3 = f32[8,3,2048]{2,1,0:T(4,128)S(1)} all-gather(f32[1,3,2048]{2,1,0:T(4,128)S(1)} %maximum_bitcast_fusion), channel_id=2, replica_groups=mesh['dp_0'=8,'dp_1'=4,'dp_2'=2,'vocab'=4] {'dp_0'}, dimensions={0}, use_global_device_ids=true | all-gather | bytes 221184 | tf_op jit(solution)/shard_map/all_gather | solution.py:50
  169.4 9.1 %all-gather.4 = f32[4,3,2048]{2,1,0:T(4,128)S(1)} all-gather(f32[1,3,2048]{2,1,0:T(4,128)S(1)} %maximum_bitcast_fusion.1), channel_id=3, replica_groups=mesh['dp_0'=8,'dp_1'=4,'dp_2'=2,'vocab'=4] {'dp_1'}, dimensions={0}, use_global_device_ids=true | all-gather | bytes 122880 | tf_op jit(solution)/shard_map/all_gather | solution.py:50
  178.7 11.2 %all-gather.5 = f32[2,3,2048]{2,1,0:T(4,128)S(1)} all-gather(f32[1,3,2048]{2,1,0:T(4,128)S(1)} %maximum_bitcast_fusion.2), channel_id=4, replica_groups=mesh['dp_0'=8,'dp_1'=4,'dp_2'=2,'vocab'=4] {'dp_2'}, dimensions={0}, use_global_device_ids=true | all-gather | bytes 73728 | tf_op jit(solution)/shard_map/all_gather | solution.py:50
  190.4 13.6 %all_to_all.27 = f32[32,1,2]{2,1,0:T(1,128)S(1)} all-to-all(f32[32,1,2]{2,1,0:T(1,128)S(1)} %broadcast_in_dim.90), channel_id=1, replica_groups=mesh['dp_0'=8,'dp_1'=4,'dp_2'=2,'vocab'=4] {'dp_0','dp_1'}, dimensions={0} | all-to-all | bytes 512 | tf_op jit(solution)/shard_map/all_to_all | solution.py:14
  204.1 0.6 broadcast_in_dim.92
  204.7 6.0 %all-to-all-start.4 = ((f32[8,32,2]{1,2,0:T(2,128)}), f32[8,32,2]{1,2,0:T(2,128)S(1)}, u32[]{:S(2)}, u32[]{:S(2)}) async-start(f32[8,32,2]{1,2,0:T(2,128)} %broadcast_in_dim.92), calls=%async_computation.4 | async-start | bytes 16384 | tf_op jit(solution)/shard_map/all_to_all | solution.py:14
  211.4 4.2 %all-to-all-done.4 = f32[8,32,2]{1,2,0:T(2,128)S(1)} async-done(((f32[8,32,2]{1,2,0:T(2,128)}), f32[8,32,2]{1,2,0:T(2,128)S(1)}, u32[]{:S(2)}, u32[]{:S(2)}) %all-to-all-start.4) | async-done | bytes 2080 | tf_op jit(solution)/shard_map/all_to_all | solution.py:14
  215.9 3.9 %sort.15 = (f32[512]{0:T(512)S(1)}, s32[512]{0:T(512)}) sort(f32[512]{0:T(512)S(1)} %reshape_reshape.3, s32[512]{0:T(512)S(1)} %iota.16), dimensions={0}, to_apply=%region_12.13 | sort | flops 4608 | bytes 8192 | tf_op jit(solution)/shard_map/jit(sort)/sort | solution.py:187
  219.8 0.7 dynamic_slice.27
  220.5 1.2 broadcast_subtract_fusion
  (79 shorter events, 4.1 us)
Async XLA Ops:
  7.2 14.1 %copy-start = (bf16[1024,1024]{1,0:T(8,128)(2,1)S(1)}, bf16[1024,1024]{1,0:T(8,128)(2,1)}, u32[]{:S(2)}) copy-start(bf16[1024,1024]{1,0:T(8,128)(2,1)} %param.17) | copy-start | bytes 6291460
  21.9 7.9 %copy-start.5 = (s32[2]{0:T(128)S(1)}, s32[2]{0:T(128)}, u32[]{:S(2)}) copy-start(s32[2]{0:T(128)} %param.14) | copy-start | bytes 28
  21.9 18.1 %copy-start.1 = (bf16[2,24,1024]{2,1,0:T(8,128)(2,1)S(1)}, bf16[2,24,1024]{2,1,0:T(8,128)(2,1)}, u32[]{:S(2)}) copy-start(bf16[2,24,1024]{2,1,0:T(8,128)(2,1)} %param.12) | copy-start | bytes 294916
  21.9 18.3 %copy-start.4 = (f32[1024]{0:T(1024)S(1)}, f32[1024]{0:T(1024)}, u32[]{:S(2)}) copy-start(f32[1024]{0:T(1024)} %param.20) | copy-start | bytes 12292
  26.2 13.7 %all-to-all-start.1 = ((f32[4,48,1024]{2,1,0:T(8,128)}), f32[4,48,1024]{2,1,0:T(8,128)S(1)}, u32[]{:S(2)}, u32[]{:S(2)}) async-start(f32[4,48,1024]{2,1,0:T(8,128)} %bitcast.306), calls=%async_computation.1 | async-start | bytes 1572864 | tf_op jit(solution)/shard_map/all_to_all | solution.py:38
  29.7 94.6 %all-gather.8.cloned.1.call-start = ((), (), s32[]{:S(2)}) async-start(), calls=%async_computation.5 | async-start | bytes 4259840 | tf_op jit(solution)/shard_map/all_gather | solution.py:172
  44.9 5.0 %copy-start.2 = (s32[2,24]{1,0:T(2,128)S(1)}, s32[2,24]{1,0:T(2,128)}, u32[]{:S(2)}) copy-start(s32[2,24]{1,0:T(2,128)} %param.13) | copy-start | bytes 580
  44.9 5.3 %copy-start.6 = (u32[256]{0:T(256)S(1)}, u32[256]{0:T(256)}, u32[]{:S(2)}) copy-start(u32[256]{0:T(256)} %constant.94) | copy-start | bytes 3076
  44.9 51.0 %all-to-all-start.2 = ((bf16[4,512,1024]{2,1,0:T(8,128)(2,1)}), bf16[4,512,1024]{2,1,0:T(8,128)(2,1)}, u32[]{:S(2)}, u32[]{:S(2)}) async-start(bf16[4,512,1024]{2,1,0:T(8,128)(2,1)} %broadcast_in_dim.83), calls=%async_computation.2 | async-start | bytes 8388608 | tf_op jit(solution)/shard_map/all_to_all | solution.py:14
  190.4 31.3 %copy-start.3 = (f32[2]{0:T(128)}, f32[2]{0:T(128)S(1)}, u32[]{:S(2)}) copy-start(f32[2]{0:T(128)S(1)} %convert_divide_fusion) | copy-start | bytes 28
  204.7 10.9 %all-to-all-start.4 = ((f32[8,32,2]{1,2,0:T(2,128)}), f32[8,32,2]{1,2,0:T(2,128)S(1)}, u32[]{:S(2)}, u32[]{:S(2)}) async-start(f32[8,32,2]{1,2,0:T(2,128)} %broadcast_in_dim.92), calls=%async_computation.4 | async-start | bytes 16384 | tf_op jit(solution)/shard_map/all_to_all | solution.py:14
Sparse Core Ops, SparseCore 0:
  41.2 83.0 all-gather.7
where the time goes:
time: 229 us
  blocking collectives  87.8 us (38%)
  waiting for transfers between devices  62.8 us (27%)
  matrix products  25.6 us (11%)
  between operations  15.7 us (7%)
  starting transfers between devices  14.6 us (6%)
  other arithmetic  14.4 us (6%)
  local copies, waits for them, and re-layouts  7.58 us (3%)
    all_gather x3, blocking collectives, all_in_one(): both, at, found = (lax.all_gather(jnp.concatenate(lines), axis), 0, {})  38.7 us
    all_gather x1, waiting for transfers between devices, on_device(): lax.all_gather(send_rows, DP, axis=0, tiled=True)  28.5 us
    all_to_all x2, blocking collectives, copy_for_each(): lax.all_to_all(jnp.broadcast_to(array[None], (length, *array.shape)), axi...  25.4 us
    all_to_all x2, waiting for transfers between devices, copy_for_each(): lax.all_to_all(jnp.broadcast_to(array[None], (length, *array.shape)), axi...  24.6 us
    unnamed x1, blocking collectives  23.7 us
    dot_general x4, matrix products, score_block(): lax.dot_general(block_part, table, (((1,), (1,)), ((), ())), preferred_el...  19.9 us
    all_to_all x2, starting transfers between devices, copy_for_each(): lax.all_to_all(jnp.broadcast_to(array[None], (length, *array.shape)), axi...  11 us
    all_to_all x1, waiting for transfers between devices, sum_at_owner(): lax.all_to_all(parts, axis, split_axis=0, concat_axis=0, tiled=True)  9.73 us
  transfers between devices with their start and end apart: 4, of which 4 were waited for; matrix products, arithmetic and copies ran while one was open for 2% of the time, Pallas kernels for 0%

commit v1 on v0

--- a/solution.py
+++ b/solution.py
@@ -7,6 +7,12 @@
 CAP = 32
 DP = ("dp_0", "dp_1", "dp_2")
 DP_VOCAB = ("dp_0", "dp_1", "dp_2", "vocab")
+
+
+def create_scenes_now(piece_in, axis_name):
+    block_last = jnp.stack([piece_in for _ in range(lax.axis_size(axis_name))], axis=0)
+    reached = lax.all_to_all(block_last, axis_name, 0, 0)
+    return jnp.concatenate(reached, axis=0)
 
 
 def copy_for_each(array, axis):
@@ -168,10 +174,7 @@
     blank_dp = jnp.zeros((dp_rows,), jnp.float32)
     peaks, sums_exp, picks = accumulate(
         (blank_dp, blank_dp, blank_dp),
-        (
-            lax.all_gather(send_rows, DP, axis=0, tiled=True),
-            lax.all_gather(send_targets, DP, axis=0, tiled=True),
-        ),
+        (create_scenes_now(send_rows, DP), lax.all_gather(send_targets, DP, axis=0, tiled=True)),
         jnp.int32(0),
     )
     peaks, sums_exp, picks = joined_all((peaks, sums_exp, picks), DP, merge_pair)

time: 229 us -> 306 us (1.34)
  blocking collectives: 87.8 us -> 179 us
  between operations: 15.7 us -> 2.25 us
  waiting for transfers between devices: 62.8 us -> 49.5 us
  starting transfers between devices: 14.6 us -> 25.6 us
    unnamed x1, blocking collectives: 23.7 us -> 97.1 us
    all_gather x1 -> x0, waiting for transfers between devices: 28.5 us -> none  [on_device(): lax.all_gather(send_rows, DP, axis=0, tiled=True)]
    all_to_all x2, waiting for transfers between devices: 24.6 us -> 49.5 us  [copy_for_each(): lax.all_to_all(jnp.broadcast_to(array[None], (length, *array.shape)), axi...]
    all_to_all x0 -> x1, blocking collectives: none -> 14 us  [sum_at_owner(): lax.all_to_all(parts, axis, split_axis=0, concat_axis=0, tiled=True)]
    all_to_all x1, starting transfers between devices: 3.49 us -> 15.5 us  [create_scenes_now(): reached = lax.all_to_all(block_last, axis_name, 0, 0)]
    all_to_all x1, waiting for transfers between devices: 9.73 us -> 0.01 us  [create_scenes_now(): reached = lax.all_to_all(block_last, axis_name, 0, 0)]
  transfers between devices with their start and end apart: 4 -> 3, of which waited for: 4 -> 2; matrix products, arithmetic and copies ran while one was open for 2% -> 1% of each run, Pallas kernels for 0% -> 0%
where the time goes in v1:
time: 306 us; the launch traced here: 305 us
  blocking collectives  179 us (58%)
  waiting for transfers between devices  49.5 us (16%)
  starting transfers between devices  25.6 us (8%)
  matrix products  24.8 us (8%)
  other arithmetic  14.4 us (5%)
  local copies, waits for them, and re-layouts  10.1 us (3%)
    unnamed x1, blocking collectives  97.1 us
    all_to_all x2, waiting for transfers between devices, copy_for_each(): lax.all_to_all(jnp.broadcast_to(array[None], (length, *array.shape)), axi...  49.5 us
    all_gather x3, blocking collectives, all_in_one(): both, at, found = (lax.all_gather(jnp.concatenate(lines), axis), 0, {})  40.7 us
    all_to_all x2, blocking collectives, copy_for_each(): lax.all_to_all(jnp.broadcast_to(array[None], (length, *array.shape)), axi...  26.9 us
    dot_general x4, matrix products, score_block(): lax.dot_general(block_part, table, (((1,), (1,)), ((), ())), preferred_el...  19.9 us
    all_to_all x1, starting transfers between devices, create_scenes_now(): reached = lax.all_to_all(block_last, axis_name, 0, 0)  15.5 us
    all_to_all x1, blocking collectives, sum_at_owner(): lax.all_to_all(parts, axis, split_axis=0, concat_axis=0, tiled=True)  14 us
    all_to_all x2, starting transfers between devices, copy_for_each(): lax.all_to_all(jnp.broadcast_to(array[None], (length, *array.shape)), axi...  10 us
  transfers between devices with their start and end apart: 3, of which 2 were waited for; matrix products, arithmetic and copies ran while one was open for 1% of the time, Pallas kernels for 0%

profile of v1, /device:TPU:1, one launch (start us, length us, event | category | flops | bytes accessed | tf_op | source)
XLA Modules:
  0.0 305.4 jit_solution(17548785909252117849)
XLA Ops:
  0.6 1.1 fusion.14
  1.9 1.0 fusion.17
  2.9 11.8 %all_to_all.31 = bf16[4,48,1024]{2,1,0:T(8,128)(2,1)S(1)} all-to-all(bf16[4,48,1024]{2,1,0:T(8,128)(2,1)S(1)} %broadcast_in_dim.82), channel_id=1, replica_groups=mesh['dp_0'=8,'dp_1'=4,'dp_2'=2,'vocab'=4] {'vocab'}, dimensions={0} | all-to-all | bytes 786432 | tf_op jit(solution)/shard_map/all_to_all | solution.py:20
  14.8 0.6 fusion.78
  15.3 4.2 %fusion.7 = f32[192,1024]{1,0:T(8,128)} fusion(bf16[1024,1024]{1,0:T(8,128)(2,1)} %param.19, bf16[192,1024]{1,0:T(8,128)(2,1)S(1)} %bitcast.305, bf16[1024,1024]{1,0:T(8,128)(2,1)} %param.18, f32[192,1024]{1,0:T(8,128)S(1)} %fusion.78), kind=kOutput, calls=%fused_computation.11 | convolution fusion | flops 806486016 | bytes 6160384 | tf_op jit(solution)/shard_map/dot_general | solution.py:154
  19.5 14.0 %all_to_all.32 = f32[4,48,1024]{2,1,0:T(8,128)S(1)} all-to-all(f32[4,48,1024]{2,1,0:T(8,128)} %bitcast.306), channel_id=1, replica_groups=mesh['dp_0'=8,'dp_1'=4,'dp_2'=2,'vocab'=4] {'vocab'}, dimensions={0} | all-to-all | bytes 1572864 | tf_op jit(solution)/shard_map/all_to_all | solution.py:44
  33.5 3.7 %broadcast_in_dim.83 = bf16[4,512,1024]{2,1,0:T(8,128)(2,1)} broadcast(bf16[512,1024]{1,0:T(8,128)(2,1)} %param.21), dimensions={1,2} | broadcast | bytes 5242880 | tf_op jit(solution)/shard_map/broadcast_in_dim | solution.py:21
  37.3 5.0 %all-to-all-start.3 = ((bf16[4,512,1024]{2,1,0:T(8,128)(2,1)}), bf16[4,512,1024]{2,1,0:T(8,128)(2,1)}, u32[]{:S(2)}, u32[]{:S(2)}) async-start(bf16[4,512,1024]{2,1,0:T(8,128)(2,1)} %broadcast_in_dim.83), calls=%async_computation.3 | async-start | bytes 8388608 | tf_op jit(solution)/shard_map/all_to_all | solution.py:20
  43.3 45.3 %all-to-all-done.3 = bf16[4,512,1024]{2,1,0:T(8,128)(2,1)} async-done(((bf16[4,512,1024]{2,1,0:T(8,128)(2,1)}), bf16[4,512,1024]{2,1,0:T(8,128)(2,1)}, u32[]{:S(2)}, u32[]{:S(2)}) %all-to-all-start.3) | async-done | bytes 4194336 | tf_op jit(solution)/shard_map/all_to_all | solution.py:20
  88.5 2.5 stack.2
  91.0 15.5 %all-to-all-start.2 = ((bf16[64,32,1024]{2,1,0:T(8,128)(2,1)}), bf16[64,32,1024]{2,1,0:T(8,128)(2,1)}, u32[]{:S(2)}, u32[]{:S(2)}) async-start(bf16[64,32,1024]{2,1,0:T(8,128)(2,1)} %stack.2), calls=%async_computation.2 | async-start | bytes 8388608 | tf_op jit(solution)/shard_map/all_to_all | solution.py:14
  106.9 0.6 dynamic-slice.1
  108.5 97.1 %all-reduce = s32[2048]{0:T(1024)S(1)} all-reduce(s32[2048]{0:T(1024)S(1)} %dynamic-update-slice), channel_id=1, replica_groups=mesh['dp_0'=8,'dp_1'=4,'dp_2'=2,'vocab'=4] {'dp_0','dp_1','dp_2'}, use_global_device_ids=true, to_apply=%add | all-reduce | flops 2048 | bytes 16384
  205.6 26.3 %while.15 = (s32[]{:T(128)}, f32[4,512]{1,0:T(4,128)S(1)}, f32[4,512]{1,0:T(4,128)S(1)}, f32[4,512]{1,0:T(4,128)S(1)}, bf16[4,512,1024]{2,1,0:T(8,128)(2,1)}, /*...) while((s32[]{:T(128)}, f32[4,512]{1,0:T(4,128)S(1)}, ...), condition=%wide.region_9.10_spmd.clone, body=%wide.region_5.9_spmd.clone.sunk | while | flops 2153774080 | bytes 13658745 | solution.py:121
  205.6 5.0 %fusion.88 = (f32[512]{0:T(512)S(1)}, f32[512,2048]{1,0:T(8,128)S(1)}) fusion(bf16[2048,1024]{1,0:T(8,128)(2,1)} %get-tuple-element.189, bf16[4,512,1024]{2,1,0:T(8,128)(2,1)} %get-tuple-element.188, s32[]{:T(128)} %get-tuple-element.174), kind=kOutput, calls=%fused_computation.138.clone.1 | convolution fusion | flops 2148531712 | bytes 9439744 | tf_op jit(solution)/shard_map/while/body/eval_jaxpr/dot_general | solution.py:107
  210.6 1.4 select_reduce_fusion.5
  212.2 5.0 %fusion.88 = (f32[512]{0:T(512)S(1)}, f32[512,2048]{1,0:T(8,128)S(1)}) fusion(bf16[2048,1024]{1,0:T(8,128)(2,1)} %get-tuple-element.189, bf16[4,512,1024]{2,1,0:T(8,128)(2,1)} %get-tuple-element.188, s32[]{:T(128)} %get-tuple-element.174), kind=kOutput, calls=%fused_computation.138.clone.1 | convolution fusion | flops 2148531712 | bytes 9439744 | tf_op jit(solution)/shard_map/while/body/eval_jaxpr/dot_general | solution.py:107
  217.2 1.4 select_reduce_fusion.5
  218.8 5.0 %fusion.88 = (f32[512]{0:T(512)S(1)}, f32[512,2048]{1,0:T(8,128)S(1)}) fusion(bf16[2048,1024]{1,0:T(8,128)(2,1)} %get-tuple-element.189, bf16[4,512,1024]{2,1,0:T(8,128)(2,1)} %get-tuple-element.188, s32[]{:T(128)} %get-tuple-element.174), kind=kOutput, calls=%fused_computation.138.clone.1 | convolution fusion | flops 2148531712 | bytes 9439744 | tf_op jit(solution)/shard_map/while/body/eval_jaxpr/dot_general | solution.py:107
  223.8 1.4 select_reduce_fusion.5
  225.4 5.0 %fusion.88 = (f32[512]{0:T(512)S(1)}, f32[512,2048]{1,0:T(8,128)S(1)}) fusion(bf16[2048,1024]{1,0:T(8,128)(2,1)} %get-tuple-element.189, bf16[4,512,1024]{2,1,0:T(8,128)(2,1)} %get-tuple-element.188, s32[]{:T(128)} %get-tuple-element.174), kind=kOutput, calls=%fused_computation.138.clone.1 | convolution fusion | flops 2148531712 | bytes 9439744 | tf_op jit(solution)/shard_map/while/body/eval_jaxpr/dot_general | solution.py:107
  230.4 1.4 select_reduce_fusion.5
  232.0 18.6 %all-gather.3 = f32[8,3,2048]{2,1,0:T(4,128)S(1)} all-gather(f32[1,3,2048]{2,1,0:T(4,128)S(1)} %maximum_bitcast_fusion), channel_id=2, replica_groups=mesh['dp_0'=8,'dp_1'=4,'dp_2'=2,'vocab'=4] {'dp_0'}, dimensions={0}, use_global_device_ids=true | all-gather | bytes 221184 | tf_op jit(solution)/shard_map/all_gather | solution.py:56
  250.9 9.4 %all-gather.4 = f32[4,3,2048]{2,1,0:T(4,128)S(1)} all-gather(f32[1,3,2048]{2,1,0:T(4,128)S(1)} %maximum_bitcast_fusion.1), channel_id=3, replica_groups=mesh['dp_0'=8,'dp_1'=4,'dp_2'=2,'vocab'=4] {'dp_1'}, dimensions={0}, use_global_device_ids=true | all-gather | bytes 122880 | tf_op jit(solution)/shard_map/all_gather | solution.py:56
  260.5 12.6 %all-gather.5 = f32[2,3,2048]{2,1,0:T(4,128)S(1)} all-gather(f32[1,3,2048]{2,1,0:T(4,128)S(1)} %maximum_bitcast_fusion.2), channel_id=4, replica_groups=mesh['dp_0'=8,'dp_1'=4,'dp_2'=2,'vocab'=4] {'dp_2'}, dimensions={0}, use_global_device_ids=true | all-gather | bytes 73728 | tf_op jit(solution)/shard_map/all_gather | solution.py:56
  273.7 15.1 %all_to_all.33 = f32[32,1,2]{2,1,0:T(1,128)S(1)} all-to-all(f32[32,1,2]{2,1,0:T(1,128)S(1)} %broadcast_in_dim.90), channel_id=1, replica_groups=mesh['dp_0'=8,'dp_1'=4,'dp_2'=2,'vocab'=4] {'dp_0','dp_1'}, dimensions={0} | all-to-all | bytes 512 | tf_op jit(solution)/shard_map/all_to_all | solution.py:20
  288.9 0.6 broadcast_in_dim.92
  289.5 5.0 %all-to-all-start.5 = ((f32[8,32,2]{1,2,0:T(2,128)}), f32[8,32,2]{1,2,0:T(2,128)S(1)}, u32[]{:S(2)}, u32[]{:S(2)}) async-start(f32[8,32,2]{1,2,0:T(2,128)} %broadcast_in_dim.92), calls=%async_computation.5 | async-start | bytes 16384 | tf_op jit(solution)/shard_map/all_to_all | solution.py:20
  295.2 4.2 %all-to-all-done.5 = f32[8,32,2]{1,2,0:T(2,128)S(1)} async-done(((f32[8,32,2]{1,2,0:T(2,128)}), f32[8,32,2]{1,2,0:T(2,128)S(1)}, u32[]{:S(2)}, u32[]{:S(2)}) %all-to-all-start.5) | async-done | bytes 2080 | tf_op jit(solution)/shard_map/all_to_all | solution.py:20
  299.7 3.9 %sort.15 = (f32[512]{0:T(512)S(1)}, s32[512]{0:T(512)}) sort(f32[512]{0:T(512)S(1)} %reshape_reshape.7, s32[512]{0:T(512)S(1)} %iota.16), dimensions={0}, to_apply=%region_12.13 | sort | flops 4608 | bytes 8192 | tf_op jit(solution)/shard_map/jit(sort)/sort | solution.py:190
  303.6 0.7 dynamic_slice.27
  304.2 1.2 broadcast_subtract_fusion
  (78 shorter events, 3.7 us)
Async XLA Ops:
  0.6 14.1 %copy-start = (bf16[1024,1024]{1,0:T(8,128)(2,1)S(1)}, bf16[1024,1024]{1,0:T(8,128)(2,1)}, u32[]{:S(2)}) copy-start(bf16[1024,1024]{1,0:T(8,128)(2,1)} %param.17) | copy-start | bytes 6291460
  37.3 5.0 %copy-start.5 = (s32[2]{0:T(128)S(1)}, s32[2]{0:T(128)}, u32[]{:S(2)}) copy-start(s32[2]{0:T(128)} %param.14) | copy-start | bytes 28
  37.3 5.5 %copy-start.1 = (bf16[2,24,1024]{2,1,0:T(8,128)(2,1)S(1)}, bf16[2,24,1024]{2,1,0:T(8,128)(2,1)}, u32[]{:S(2)}) copy-start(bf16[2,24,1024]{2,1,0:T(8,128)(2,1)} %param.12) | copy-start | bytes 294916
  37.3 5.8 %copy-start.4 = (f32[1024]{0:T(1024)S(1)}, f32[1024]{0:T(1024)}, u32[]{:S(2)}) copy-start(f32[1024]{0:T(1024)} %param.20) | copy-start | bytes 12292
  37.3 51.3 %all-to-all-start.3 = ((bf16[4,512,1024]{2,1,0:T(8,128)(2,1)}), bf16[4,512,1024]{2,1,0:T(8,128)(2,1)}, u32[]{:S(2)}, u32[]{:S(2)}) async-start(bf16[4,512,1024]{2,1,0:T(8,128)(2,1)} %broadcast_in_dim.83), calls=%async_computation.3 | async-start | bytes 8388608 | tf_op jit(solution)/shard_map/all_to_all | solution.py:20
  91.0 15.6 %copy-start.2 = (s32[2,24]{1,0:T(2,128)S(1)}, s32[2,24]{1,0:T(2,128)}, u32[]{:S(2)}) copy-start(s32[2,24]{1,0:T(2,128)} %param.13) | copy-start | bytes 580
  91.0 15.8 %copy-start.6 = (u32[256]{0:T(256)S(1)}, u32[256]{0:T(256)}, u32[]{:S(2)}) copy-start(u32[256]{0:T(256)} %constant.94) | copy-start | bytes 3076
  91.0 114.6 %all-to-all-start.2 = ((bf16[64,32,1024]{2,1,0:T(8,128)(2,1)}), bf16[64,32,1024]{2,1,0:T(8,128)(2,1)}, u32[]{:S(2)}, u32[]{:S(2)}) async-start(bf16[64,32,1024]{2,1,0:T(8,128)(2,1)} %stack.2), calls=%async_computation.2 | async-start | bytes 8388608 | tf_op jit(solution)/shard_map/all_to_all | solution.py:14
  273.7 31.8 %copy-start.3 = (f32[2]{0:T(128)}, f32[2]{0:T(128)S(1)}, u32[]{:S(2)}) copy-start(f32[2]{0:T(128)S(1)} %convert_divide_fusion) | copy-start | bytes 28
  289.5 9.9 %all-to-all-start.5 = ((f32[8,32,2]{1,2,0:T(2,128)}), f32[8,32,2]{1,2,0:T(2,128)S(1)}, u32[]{:S(2)}, u32[]{:S(2)}) async-start(f32[8,32,2]{1,2,0:T(2,128)} %broadcast_in_dim.92), calls=%async_computation.5 | async-start | bytes 16384 | tf_op jit(solution)/shard_map/all_to_all | solution.py:20
